TPU v7x, 256 devices: a whole 4x4x8 slice. The times are simulated.
256 devices in a mesh: seg: 4 (over x_lo, core), ops: 64 (over x_hi, y, z).
Axes of the slice: x: 4 (x_hi: 2, x_lo: 2; x = x_hi * 2 + x_lo), y: 4, z: 8, core: 2. Of those that a mesh axis runs over, the one named last changes fastest.
Arguments:
- amat: bfloat16 [16384, 128], P(('seg', 'ops')), may hold values from -6 to 6
- lam: float32 [16384], P(('seg', 'ops')), may hold values from 0.3 to 3
- hdiag: float32 [16384, 128], P(('seg', 'ops')), may hold values from 0.25 to 8
- left_ops: bfloat16 [4, 384, 4096, 128], P('seg', 'ops'), may hold values from -0.5 to 0.5
- right_operators: bfloat16 [4, 384, 4096, 128], P('seg', 'ops'), may hold values from -0.02734375 to 0.02734375
- couple: int32 [4, 384, 32], P('seg', 'ops'), may hold values from 0 to 31
- blockmask: int32 [4, 384, 32], P('seg', 'ops'), may hold values 0 or 1
Outputs:
- sigma_two: float32 [16384, 128], P(('seg', 'ops'))
- theta: float32 [4], P('seg')
Inputs may be any that keep to these rules, and one draw needn't show every extreme that they name: couple[s, k, i] is the sector of the vector that term k of segment s carries into sector i.
All inputs are finite; a program needn't handle non-finite values. No bound on the sum of `blockmask` on one device may be relied on, other than what follows from the above.
Results may differ from a plain program's by a relative error of at most 0.009.
Values may be sent and summed in bfloat16 or wider, within the bound.
A program may use at most 64 MiB of HBM per device.

v0:
```python
from functools import partial

import jax
import jax.numpy as jnp
from jax import lax
from jax.sharding import PartitionSpec as P


def shifted(array, axis, by):
    devices = lax.axis_size(axis)
    pairs = [(i, i + by) for i in range(devices) if 0 <= i + by < devices]
    return lax.ppermute(array, axis, pairs)


def copy_for_each(array, axis):
    devices = lax.axis_size(axis)
    return lax.all_to_all(
        jnp.broadcast_to(array[None], (devices, *array.shape)), axis, 0, 0, tiled=True
    )


def in_order(tiles, dim):
    tiles = jnp.moveaxis(tiles, 0, dim)
    lengths = tiles.shape
    return tiles.reshape(*lengths[:dim], lengths[dim] * lengths[dim + 1], *lengths[dim + 2 :])


def collect(array, axis, dim):
    tiles = copy_for_each(array, axis)
    return in_order(tiles, dim)


def split_up(array, dim, devices):
    before, after = (array.shape[:dim], array.shape[dim + 1 :])
    return jnp.moveaxis(array.reshape(*before, devices, -1, *after), dim, 0)


def summed_on_arrival(array, axis, dim):
    devices = lax.axis_size(axis)
    tiles = lax.all_to_all(split_up(array, dim, devices), axis, 0, 0, tiled=True)
    return jnp.sum(tiles, axis=0)


def taken_together(array, axis):
    everything = copy_for_each(array, axis)
    return jnp.sum(everything, axis=0)


def packed_total(arrays, axis):
    ends = [0]
    for a in arrays:
        ends.append(ends[-1] + a.size)
    running = taken_together(jnp.concatenate([a.ravel() for a in arrays]), axis)
    return tuple((running[b:e].reshape(a.shape) for a, b, e in zip(arrays, ends, ends[1:])))


def row_per_term(blocks, left, right, links, live, width, start, count):
    nterms = left.shape[0]
    nblock = max(count // width, 1)
    inside = min(count, width)
    lrows = left.reshape(nterms, nblock, inside, width)
    rblock = right.reshape(nterms, nblock, width, width)
    picked = blocks[links]
    inner_block = jnp.einsum("knra,knab->knrb", lrows, picked, preferred_element_type=jnp.float32)
    inner_block = (inner_block * live[:, :, None, None]).astype(jnp.bfloat16)
    result = jnp.einsum("knrb,kndb->nrd", inner_block, rblock, preferred_element_type=jnp.float32)
    return result.reshape(count, width)


def body(amat, lam, hdiag, left_ops, right_operators, couple, blockmask):
    width = amat.shape[1]
    links = couple[0]
    nsector = links.shape[1]
    bond = width * nsector
    left = left_ops[0]
    right = right_operators[0]
    live = blockmask[0].astype(jnp.float32)
    segment = lax.axis_index("seg")
    earlier = shifted(lam, "seg", 1)
    weights = jnp.where(segment == 0, jnp.ones_like(earlier), earlier)
    psi = (weights[:, None] * amat.astype(jnp.float32)).astype(jnp.bfloat16)

    def apply_terms(vector):
        whole = collect(vector, "ops", 0)
        blocks = whole.reshape(nsector, width, width)
        rows_of = partial(row_per_term, blocks, left, right, links, live, width)
        summed = summed_on_arrival(rows_of(0, bond), "ops", 0)
        return summed + hdiag * vector.astype(jnp.float32)

    sigma_one = apply_terms(psi)
    psi_float = psi.astype(jnp.float32)
    numer, denom = packed_total(
        (jnp.sum(psi_float * sigma_one), jnp.sum(psi_float * psi_float)), "ops"
    )
    quotient = numer / denom
    correction = ((sigma_one - quotient * psi_float) / hdiag).astype(jnp.bfloat16)
    sigma_two = apply_terms(correction)
    return (sigma_two, quotient.reshape(1))


def solution(mesh):
    placed = (
        P(("seg", "ops"), None),
        P(("seg", "ops")),
        P(("seg", "ops"), None),
        P("seg", "ops", None, None),
        P("seg", "ops", None, None),
        P("seg", "ops", None),
        P("seg", "ops", None),
    )
    return jax.shard_map(
        body,
        mesh=mesh,
        in_specs=placed,
        out_specs=(P(("seg", "ops"), None), P("seg")),
        check_vma=False,
    )
```

profile of v0, /device:TPU:32, one launch (start us, length us, event | category | flops | bytes accessed | tf_op | source)
XLA Modules:
  0.0 262.0 jit_solution(5359676101618231503)
XLA Ops:
  0.6 1.7 collective-permute-start
  2.4 0.9 collective-permute-done
  3.3 0.8 multiply_convert_fusion.2
  4.1 1.2 broadcast_in_dim.9
  5.4 14.2 %all-to-all-start = ((bf16[64,64,128]{2,1,0:T(8,128)(2,1)}), bf16[64,64,128]{2,1,0:T(8,128)(2,1)S(1)}, u32[]{:S(2)}, u32[]{:S(2)}) async-start(bf16[64,64,128]{2,1,0:T(8,128)(2,1)} %broadcast_in_dim.9), calls=%async_computation | async-start | bytes 2097152 | tf_op jit(solution)/shard_map/all_to_all | solution.py:17
  19.6 0.7 convert_element_type.40
  20.3 0.7 fusion.38
  21.0 0.1 reshape.62
  21.1 0.1 copy.40
  21.1 29.4 %all-to-all-done = bf16[64,64,128]{2,1,0:T(8,128)(2,1)S(1)} async-done(((bf16[64,64,128]{2,1,0:T(8,128)(2,1)}), bf16[64,64,128]{2,1,0:T(8,128)(2,1)S(1)}, u32[]{:S(2)}, u32[]{:S(2)}) %all-to-all-start) | async-done | bytes 1048608 | tf_op jit(solution)/shard_map/all_to_all | solution.py:17
  50.6 8.0 %gather_fusion = bf16[192,128,128]{2,1,0:T(8,128)(2,1)} fusion(bf16[32,128,128]{2,1,0:T(8,128)(2,1)S(1)} %bitcast.26, s32[1024]{0:T(1024)S(1)} %pad_clamp_fusion), kind=kCustom, calls=%fused_computation | custom fusion | bytes 12583680 | tf_op jit(solution)/shard_map/gather | solution.py:63
  58.6 11.0 %fusion.1 = f32[32,128,128,1]{2,1,3,0:T(8,128)} fusion(f32[6,32]{0,1:T(8,128)S(1)} %bitcast.32, bf16[6,32,128,128]{3,2,1,0:T(8,128)(2,1)} %bitcast.34, bf16[6,32,128,128]{3,2,1,0:T(8,128)(2,1)} %bitcast.29, bf16[6,32,128,128]{3,2,1,0:T(8,128)(2,1)} %bitcast.36), kind=kOutput, calls=%fused_computation.5 | convolution fusion | flops 1616904192 | bytes 20972288 | tf_op jit(solution)/shard_map/knrb,kndb->nrd/dot_general | solution.py:66
  69.6 0.0 copy-start
  69.6 0.0 copy-start.1
  69.6 59.1 %all_to_all.26 = f32[64,64,128]{2,1,0:T(8,128)S(1)} all-to-all(f32[64,64,128]{2,1,0:T(8,128)} %bitcast.31), channel_id=1, replica_groups=mesh['seg'=4,'ops'=64] {'ops'}, dimensions={0} | all-to-all | bytes 4194304 | tf_op jit(solution)/shard_map/all_to_all | solution.py:40
  128.6 0.1 reduce_sum.45
  128.8 0.0 copy-done
  128.8 0.0 copy-done.1
  128.8 0.7 fusion.33
  129.5 1.4 pad_maximum_fusion
  130.9 18.0 %all_to_all.27 = f32[64,1,2]{2,1,0:T(1,128)S(1)} all-to-all(f32[64,1,2]{2,1,0:T(1,128)S(1)} %broadcast_in_dim.10), channel_id=1, replica_groups=mesh['seg'=4,'ops'=64] {'ops'}, dimensions={0} | all-to-all | bytes 1024 | tf_op jit(solution)/shard_map/all_to_all | solution.py:17
  148.9 0.1 reduce_sum.48
  149.0 0.6 fusion.39
  150.9 0.1 fusion.37
  151.0 0.2 broadcast_in_dim.11
  151.2 33.9 %all_to_all.28 = bf16[64,64,128]{2,1,0:T(8,128)(2,1)S(1)} all-to-all(bf16[64,64,128]{2,1,0:T(8,128)(2,1)S(1)} %broadcast_in_dim.11), channel_id=1, replica_groups=mesh['seg'=4,'ops'=64] {'ops'}, dimensions={0} | all-to-all | bytes 2097152 | tf_op jit(solution)/shard_map/all_to_all | solution.py:17
  185.1 8.0 %gather_fusion.1 = bf16[192,128,128]{2,1,0:T(8,128)(2,1)} fusion(bf16[32,128,128]{2,1,0:T(8,128)(2,1)S(1)} %bitcast.27, s32[1024]{0:T(1024)S(1)} %pad_clamp_fusion), kind=kCustom, calls=%fused_computation.1 | custom fusion | bytes 12583680 | tf_op jit(solution)/shard_map/gather | solution.py:63
  193.1 11.0 %fusion.4 = f32[32,128,128,1]{2,1,3,0:T(8,128)} fusion(f32[6,32]{0,1:T(8,128)S(1)} %bitcast.33, bf16[6,32,128,128]{3,2,1,0:T(8,128)(2,1)} %bitcast.35, bf16[6,32,128,128]{3,2,1,0:T(8,128)(2,1)} %bitcast.28, bf16[6,32,128,128]{3,2,1,0:T(8,128)(2,1)} %bitcast.37), kind=kOutput, calls=%fused_computation.7 | convolution fusion | flops 1616904192 | bytes 20972288 | tf_op jit(solution)/shard_map/knrb,kndb->nrd/dot_general | solution.py:66
  204.1 56.0 %all_to_all.29 = f32[64,64,128]{2,1,0:T(8,128)S(1)} all-to-all(f32[64,64,128]{2,1,0:T(8,128)} %bitcast.30), channel_id=1, replica_groups=mesh['seg'=4,'ops'=64] {'ops'}, dimensions={0} | all-to-all | bytes 4194304 | tf_op jit(solution)/shard_map/all_to_all | solution.py:40
  260.1 0.1 reduce_sum.49
  260.2 0.6 multiply_add_fusion
  (3 shorter events, 0.0 us)
Async XLA Ops:
  0.6 2.7 %collective-permute-start = (f32[64]{0:T(128)}, f32[64]{0:T(128)S(1)}, u32[]{:S(2)}, u32[]{:S(2)}) collective-permute-start(f32[64]{0:T(128)} %param.8), channel_id=1, source_target_pairs={{0,64},{64,128},{128,192},{1,65},{65,129},{129,193},{2,66},{66,130... | collective-permute-start | bytes 776 | tf_op jit(solution)/shard_map/ppermute | solution.py:12
  5.4 45.2 %all-to-all-start = ((bf16[64,64,128]{2,1,0:T(8,128)(2,1)}), bf16[64,64,128]{2,1,0:T(8,128)(2,1)S(1)}, u32[]{:S(2)}, u32[]{:S(2)}) async-start(bf16[64,64,128]{2,1,0:T(8,128)(2,1)} %broadcast_in_dim.9), calls=%async_computation | async-start | bytes 2097152 | tf_op jit(solution)/shard_map/all_to_all | solution.py:17
  69.6 59.2 %copy-start = (f32[64,128]{1,0:T(8,128)S(1)}, f32[64,128]{1,0:T(8,128)}, u32[]{:S(2)}) copy-start(f32[64,128]{1,0:T(8,128)} %param.9) | copy-start | bytes 98308
  69.6 59.2 %copy-start.1 = (bf16[64,128]{1,0:T(8,128)(2,1)S(1)}, bf16[64,128]{1,0:T(8,128)(2,1)}, u32[]{:S(2)}) copy-start(bf16[64,128]{1,0:T(8,128)(2,1)} %param.7) | copy-start | bytes 49156
where the time goes:
time: 263 us; the launch traced here: 262 us
  blocking collectives  167 us (63%)
  waiting for transfers between devices  30.4 us (12%)
  matrix products  21.9 us (8%)
  local copies, waits for them, and re-layouts  18.4 us (7%)
  starting transfers between devices  16 us (6%)
  other arithmetic  5.31 us (2%)
  between operations  3.16 us (1%)
    all_to_all x2, blocking collectives, summed_on_arrival(): lax.all_to_all(split_up(array, dim, devices), axis, 0, 0, tiled=True)  115 us
    all_to_all x2, blocking collectives, copy_for_each(): lax.all_to_all(jnp.broadcast_to(array[None], (devices, *array.shape)), ax...  51.9 us
    all_to_all x1, waiting for transfers between devices, copy_for_each(): lax.all_to_all(jnp.broadcast_to(array[None], (devices, *array.shape)), ax...  29.4 us
    dot_general x2, matrix products, row_per_term(): jnp.einsum('knrb,kndb->nrd', inner_block, rblock, preferred_element_type=...  21.9 us
    gather x2, local copies, waits for them, and re-layouts, row_per_term(): picked = blocks[links]  16.1 us
    all_to_all x1, starting transfers between devices, copy_for_each(): lax.all_to_all(jnp.broadcast_to(array[None], (devices, *array.shape)), ax...  14.2 us
  transfers between devices with their start and end apart: 2, of which 2 were waited for; matrix products, arithmetic and copies ran while one was open for 1% of the time, Pallas kernels for 0%

commit v1 on v0

v1 whole, which is shorter than its diff:
```python
import functools

import jax
import jax.numpy as jnp
from jax import lax
from jax.experimental import pallas as pl
from jax.experimental.pallas import tpu as pltpu
from jax.sharding import PartitionSpec as P

NX, NY, NZ = 2, 4, 8
NXZ = NX * NZ
NSEG = 4
NQ, BS, ROWS = 32, 128, 64
UNIT = 4
LAG = 6
F32, BF16 = jnp.float32, jnp.bfloat16


def kernel(amat_h, lam_h, hdiag_h, left_h, right_h, couple, mask,
           out, theta_out,
           amat, lam, hdiag, left, right, lam_in, v, opp_send, near_send,
           opp_in, near_in, own_acc, plane_send, plane_in, sigma,
           numer, denom, numer_y, numer_p,
           load_sem, lam_sem, op_sem, lam_send, plane_s, plane_r,
           ring_s, ring_r, last_s, last_r, sum_s, sum_r, psum_s, psum_r,
           num_s, num_r, nump_s, nump_r):
    nterms = left.shape[0]
    seg = lax.axis_index("seg")
    me = lax.axis_index("ops")
    x, y, z = me // (NY * NZ), (me // NZ) % NY, me % NZ
    xz = x * NZ + z
    up, down, across = (y + 1) % NY, (y + 3) % NY, (y + 2) % NY

    def device(tx, ty, tz):
        return tx * (NY * NZ) + ty * NZ + tz

    def place(p):
        q = p // 2
        dz = (q % 2) * ((q + 1) // 2) + (1 - q % 2) * (NZ - q // 2)
        return (x + p) % NX, (z + dz) % NZ

    def piece(ref, o):
        return ref.at[o // 2, pl.ds(pl.multiple_of((o % 2) * ROWS, ROWS), ROWS), :]

    def remote(src, dst, s, r, target, axis="ops"):
        return pltpu.make_async_remote_copy(
            src_ref=src, dst_ref=dst, send_sem=s, recv_sem=r,
            device_id={axis: target}, device_id_type=pl.DeviceIdType.MESH)

    small = [pltpu.make_async_copy(amat_h, amat, load_sem.at[0]),
             pltpu.make_async_copy(lam_h, lam, load_sem.at[1]),
             pltpu.make_async_copy(hdiag_h, hdiag, load_sem.at[2])]
    for copy in small:
        copy.start()

    def operator_copies(k):
        return (pltpu.make_async_copy(left_h.at[k], left.at[k], op_sem.at[0, k]),
                pltpu.make_async_copy(right_h.at[k], right.at[k], op_sem.at[1, k]))

    for k in range(nterms):
        for copy in operator_copies(k):
            copy.start()

    barrier = pltpu.get_barrier_semaphore()

    def greet(p, c):
        tx, tz = place(p)
        pl.semaphore_signal(barrier, inc=1, device_id={"ops": device(tx, y, tz)},
                            device_id_type=pl.DeviceIdType.MESH)
        return c

    lax.fori_loop(1, NXZ, greet, 0)
    for other in (up, down, across):
        pl.semaphore_signal(barrier, inc=1, device_id={"ops": device(x, other, z)},
                            device_id_type=pl.DeviceIdType.MESH)
    for step in (1, NSEG - 1):
        pl.semaphore_signal(barrier, inc=1, device_id={"seg": (seg + step) % NSEG},
                            device_id_type=pl.DeviceIdType.MESH)
    for copy in small:
        copy.wait()
    v[0, NQ] = jnp.zeros((BS, BS), BF16)
    v[1, NQ] = jnp.zeros((BS, BS), BF16)
    numer[...] = jnp.zeros_like(numer)
    denom[...] = jnp.zeros_like(denom)
    pl.semaphore_wait(barrier, NXZ - 1 + 3 + 2)

    pass_lam = remote(lam, lam_in, lam_send, lam_sem, (seg + 1) % NSEG, "seg")
    pass_lam.start()
    pass_lam.wait_recv()
    square = (ROWS, ROWS)
    diagonal = lax.broadcasted_iota(jnp.int32, square, 0) == lax.broadcasted_iota(jnp.int32, square, 1)
    earlier = jnp.sum(jnp.where(diagonal, jnp.broadcast_to(lam_in[...], square), 0.0), axis=1, keepdims=True)
    weights = jnp.where(seg == 0, jnp.ones_like(earlier), earlier)
    psi = (weights * amat[...].astype(F32)).astype(BF16)

    mine = (me // 2, pl.ds(pl.multiple_of((me % 2) * ROWS, ROWS), ROWS))

    def gather(s, value):
        vec = v.at[s]
        v[s, mine[0], mine[1], :] = value

        def scatter_copy(p):
            tx, tz = place(p)
            return remote(piece(vec, me), piece(vec, me), plane_s.at[p], plane_r.at[s, xz],
                          device(tx, y, tz))

        def arrival(p, ty, sem):
            tx, tz = place(p)
            where = piece(vec, device(tx, ty, tz))
            return remote(where, where, plane_s.at[p], sem.at[s, tx * NZ + tz], device(x, up, z))

        def pass_up(p):
            tx, tz = place(p)
            where = piece(vec, device(tx, y, tz))
            return remote(where, where, ring_s.at[0, p], ring_r.at[0, s, tx * NZ + tz], device(x, up, z))

        def pass_down(p):
            tx, tz = place(p)
            where = piece(vec, device(tx, y, tz))
            return remote(where, where, ring_s.at[1, p], ring_r.at[1, s, tx * NZ + tz], device(x, down, z))

        def on_up(p):
            tx, tz = place(p)
            where = piece(vec, device(tx, down, tz))
            return remote(where, where, last_s.at[p], last_r.at[s, tx * NZ + tz], device(x, up, z))

        def on_down(p):
            tx, tz = place(p)
            where = piece(vec, device(tx, up, tz))
            return remote(where, where, last_s.at[p], last_r.at[s, tx * NZ + tz], device(x, down, z))

        def first(p, c):
            scatter_copy(p).start()
            return c

        lax.fori_loop(1, NXZ, first, 0)

        def hop(p, c):
            @pl.when(p < NXZ)
            def _():
                @pl.when(p > 0)
                def _():
                    arrival(p, y, plane_r).wait_recv()
                pass_up(p).start()
                pass_down(p).start()

            @pl.when(p >= LAG)
            def _():
                q = p - LAG

                @pl.when((q // 2) % 2 == 0)
                def _():
                    arrival(q, down, ring_r.at[0]).wait_recv()
                    on_up(q).start()

                @pl.when((q // 2) % 2 == 1)
                def _():
                    arrival(q, up, ring_r.at[1]).wait_recv()
                    on_down(q).start()
            return c

        lax.fori_loop(0, NXZ + LAG, hop, 0)

        def finish(p, c):
            @pl.when((p // 2) % 2 == 0)
            def _():
                arrival(p, up, ring_r.at[1]).wait_recv()

            @pl.when((p // 2) % 2 == 1)
            def _():
                arrival(p, down, ring_r.at[0]).wait_recv()

            arrival(p, across, last_r).wait_recv()
            return c

        lax.fori_loop(0, NXZ, finish, 0)

        def sent(p, c):
            @pl.when(p > 0)
            def _():
                scatter_copy(p).wait_send()
            pass_up(p).wait_send()
            pass_down(p).wait_send()
            on_up(p).wait_send()
            return c

        return functools.partial(lax.fori_loop, 0, NXZ, sent, 0)

    contract = (((1,), (1,)), ((), ()))

    def block(s, i):
        inner = []
        for k in range(nterms):
            live = mask[k, i]
            j = couple[k, i] * live + NQ * (1 - live)
            inner.append(jnp.dot(left[k, i], v[s, j], preferred_element_type=F32).astype(BF16))
        total = None
        for k in range(0, nterms, 2):
            pair = jnp.concatenate(inner[k:k + 2], axis=1)
            rpair = jnp.concatenate([right[k, i], right[k + 1, i]], axis=1)
            part = lax.dot_general(pair, rpair, contract, preferred_element_type=F32)
            total = part if total is None else total + part
        if s == 0:
            here = v[s, i].astype(F32)
            numer[...] += jnp.sum((total * here).reshape(BS // 8, 8, BS), axis=0)
            denom[...] += jnp.sum((here * here).reshape(BS // 8, 8, BS), axis=0)
        return total

    def unit(s, half, ty, keep):
        base = half * (NQ // 2) + ty * UNIT

        def step(b, c):
            for b2 in range(2):
                keep(2 * b + b2, block(s, base + 2 * b + b2))
            return c

        lax.fori_loop(0, UNIT // 2, step, 0)

    def reduce(s):
        sends = []

        def send(src, dst, index, target):
            copy = remote(src, dst, sum_s.at[index], sum_r.at[s, index], device(x, target, z))
            copy.start()
            sends.append(copy)

        def got(dst, index):
            remote(dst, dst, sum_s.at[index], sum_r.at[s, index], device(x, up, z)).wait_recv()

        def to(ref, *at):
            def keep(b, total):
                ref[(*at, b)] = total.astype(ref.dtype)
            return keep

        def plus(ref, add, at, add_at):
            def keep(b, total):
                ref[(*at, b)] = (total + add[(*add_at, b)].astype(F32)).astype(ref.dtype)
            return keep

        unit(s, 0, across, to(opp_send, 0))
        send(opp_send.at[0], opp_in.at[s, 0], 0, up)
        unit(s, 1, across, to(opp_send, 1))
        send(opp_send.at[1], opp_in.at[s, 1], 1, down)
        unit(s, 1, up, to(near_send, 0, 1))
        send(near_send.at[0, 1], near_in.at[s, 0, 1], 2, up)
        unit(s, 0, down, to(near_send, 1, 0))
        send(near_send.at[1, 0], near_in.at[s, 1, 0], 3, down)
        got(opp_in.at[s, 0], 0)
        unit(s, 0, up, plus(near_send, opp_in, (0, 0), (s, 0)))
        send(near_send.at[0, 0], near_in.at[s, 0, 0], 4, up)
        got(opp_in.at[s, 1], 1)
        unit(s, 1, down, plus(near_send, opp_in, (1, 1), (s, 1)))
        send(near_send.at[1, 1], near_in.at[s, 1, 1], 5, down)
        unit(s, 0, y, to(own_acc, 0))
        unit(s, 1, y, to(own_acc, 1))

        if s == 0:
            own = psi.astype(F32)
            numer[...] += jnp.sum((hdiag[...] * own * own).reshape(ROWS // 8, 8, BS), axis=0)
            numer_y[y] = numer[...]
            for n, other in enumerate((up, down, across)):
                copy = remote(numer, numer_y.at[y], num_s.at[n], num_r.at[y], device(x, other, z))
                copy.start()
                sends.append(copy)

        def plane_copy(half, t):
            o = half * NZ + t
            return remote(plane_send.at[half, t], plane_in.at[s, xz], psum_s.at[o], psum_r.at[s, xz],
                          device(half, y, t))

        for half in range(2):
            got(near_in.at[s, 0, half], 4 if half == 0 else 2)
            got(near_in.at[s, 1, half], 3 if half == 0 else 5)

            def add(b, c):
                total = (own_acc[half, b] + near_in[s, 0, half, b].astype(F32)
                         + near_in[s, 1, half, b].astype(F32))
                own_acc[half, b] = total
                plane_send[half, 2 * b] = total[:ROWS].astype(BF16)
                plane_send[half, 2 * b + 1] = total[ROWS:].astype(BF16)
                return c

            lax.fori_loop(0, UNIT, add, 0)

            def go(t, c):
                @pl.when(half * NZ + t != xz)
                def _():
                    plane_copy(half, t).start()
                return c

            lax.fori_loop(0, NZ, go, 0)

        if s == 0:
            for other in (up, down, across):
                remote(numer, numer_y.at[other], num_s.at[0], num_r.at[other], device(x, up, z)).wait_recv()
            numer_p[xz] = (numer_y[0] + numer_y[1]) + (numer_y[2] + numer_y[3])

            def numer_copy(p):
                tx, tz = place(p)
                return remote(numer_p.at[xz], numer_p.at[xz], nump_s.at[p], nump_r.at[xz], device(tx, y, tz))

            def go_numer(p, c):
                numer_copy(p).start()
                return c

            lax.fori_loop(1, NXZ, go_numer, 0)

        sigma[...] = own_acc[x, z // 2, pl.ds(pl.multiple_of((z % 2) * ROWS, ROWS), ROWS), :]

        def take(p, c):
            tx, tz = place(p)
            o = tx * NZ + tz
            remote(plane_in.at[s, o], plane_in.at[s, o], psum_s.at[0], psum_r.at[s, o],
                   device(x, up, z)).wait_recv()
            sigma[...] += plane_in[s, o].astype(F32)
            return c

        lax.fori_loop(1, NXZ, take, 0)

        if s == 0:
            def take_numer(p, c):
                tx, tz = place(p)
                o = tx * NZ + tz
                remote(numer_p.at[o], numer_p.at[o], nump_s.at[0], nump_r.at[o], device(x, up, z)).wait_recv()
                return c

            lax.fori_loop(1, NXZ, take_numer, 0)

        def drain():
            for copy in sends:
                copy.wait_send()

            def sent(o, c):
                @pl.when(o != xz)
                def _():
                    plane_copy(o // NZ, o % NZ).wait_send()
                return c

            lax.fori_loop(0, NXZ, sent, 0)
            if s == 0:
                def sent_numer(p, c):
                    numer_copy(p).wait_send()
                    return c

                lax.fori_loop(1, NXZ, sent_numer, 0)

        return drain

    sent_psi = gather(0, psi)
    for k in range(nterms):
        for copy in operator_copies(k):
            copy.wait()
    drain_one = reduce(0)
    psi_float = psi.astype(F32)
    sigma_one = sigma[...] + hdiag[...] * psi_float
    top = jnp.sum(jnp.sum(numer_p[...], axis=0), keepdims=True)
    quotient = top / jnp.sum(denom[...], keepdims=True)
    correction = ((sigma_one - quotient * psi_float) / hdiag[...]).astype(BF16)
    sent_psi()
    sent_correction = gather(1, correction)
    drain_one()
    theta_out[0] = quotient[0, 0]
    pass_lam.wait_send()
    drain_two = reduce(1)
    out[...] = sigma[...] + hdiag[...] * correction.astype(F32)
    sent_correction()
    drain_two()


def body(amat, lam, hdiag, left_ops, right_operators, couple, blockmask):
    terms = left_ops.shape[1]
    vmem, dma = pltpu.VMEM, pltpu.SemaphoreType.DMA
    anywhere = pl.BlockSpec(memory_space=pl.ANY)
    scalars = pl.BlockSpec(memory_space=pltpu.SMEM)
    scratch = [
        vmem((ROWS, BS), BF16), vmem((1, ROWS), F32), vmem((ROWS, BS), F32),
        vmem((terms, NQ, BS, BS), BF16), vmem((terms, NQ, BS, BS), BF16),
        vmem((1, ROWS), F32),
        vmem((2, NQ + 1, BS, BS), BF16),
        vmem((2, UNIT, BS, BS), BF16), vmem((2, 2, UNIT, BS, BS), BF16),
        vmem((2, 2, UNIT, BS, BS), BF16), vmem((2, 2, 2, UNIT, BS, BS), BF16),
        vmem((2, UNIT, BS, BS), F32),
        vmem((2, NZ, ROWS, BS), BF16), vmem((2, NXZ, ROWS, BS), BF16),
        vmem((ROWS, BS), F32),
        vmem((8, BS), F32), vmem((8, BS), F32),
        vmem((NY, 8, BS), F32), vmem((NXZ, 8, BS), F32),
        dma((3,)), dma, dma((2, terms)), dma,
        dma((NXZ,)), dma((2, NXZ)),
        dma((2, NXZ)), dma((2, 2, NXZ)),
        dma((NXZ,)), dma((2, NXZ)),
        dma((6,)), dma((2, 6)),
        dma((NXZ,)), dma((2, NXZ)),
        dma((3,)), dma((NY,)),
        dma((NXZ,)), dma((NXZ,)),
    ]
    sigma_two, theta = pl.pallas_call(
        kernel,
        out_shape=(jax.ShapeDtypeStruct((ROWS, BS), F32), jax.ShapeDtypeStruct((1,), F32)),
        in_specs=[anywhere] * 5 + [scalars] * 2,
        out_specs=(pl.BlockSpec(memory_space=pltpu.VMEM), scalars),
        scratch_shapes=scratch,
        compiler_params=pltpu.CompilerParams(collective_id=0, has_side_effects=True),
    )(amat, lam.reshape(1, ROWS), hdiag,
      left_ops.reshape(terms, NQ, BS, BS), right_operators.reshape(terms, NQ, BS, BS),
      couple[0], blockmask[0])
    return sigma_two, theta


def solution(mesh):
    placed = (
        P(("seg", "ops"), None),
        P(("seg", "ops")),
        P(("seg", "ops"), None),
        P("seg", "ops", None, None),
        P("seg", "ops", None, None),
        P("seg", "ops", None),
        P("seg", "ops", None),
    )
    return jax.shard_map(
        body,
        mesh=mesh,
        in_specs=placed,
        out_specs=(P(("seg", "ops"), None), P("seg")),
        check_vma=False,
    )
```

time: 263 us -> 97.6 us (0.37)
  blocking collectives: 167 us -> 0 us
  Pallas kernels: 0 us -> 92.3 us
  waiting for transfers between devices: 30.4 us -> 0 us
  matrix products: 21.9 us -> 0 us
  starting transfers between devices: 16 us -> 0 us
  local copies, waits for them, and re-layouts: 18.4 us -> 2.67 us
  other arithmetic: 5.31 us -> 0 us
    all_to_all x4 -> x0, blocking collectives: 167 us -> none  [the longest x2 115 us: summed_on_arrival(): lax.all_to_all(split_up(array, dim, devices), axis, 0, 0, tiled=True)]
    pallas_call x0 -> x1, Pallas kernels: none -> 92.3 us  [body(): pl.pallas_call(kernel, out_shape=(jax.ShapeDtypeStruct((ROWS, BS), F32),...]
    all_to_all x1 -> x0, waiting for transfers between devices: 29.4 us -> none  [copy_for_each(): lax.all_to_all(jnp.broadcast_to(array[None], (devices, *array.shape)), ax...]
    dot_general x2 -> x0, matrix products: 21.9 us -> none  [row_per_term(): jnp.einsum('knrb,kndb->nrd', inner_block, rblock, preferred_element_type=...]
    gather x2 -> x0, local copies, waits for them, and re-layouts: 16.1 us -> none  [row_per_term(): picked = blocks[links]]
    all_to_all x1 -> x0, starting transfers between devices: 14.2 us -> none  [copy_for_each(): lax.all_to_all(jnp.broadcast_to(array[None], (devices, *array.shape)), ax...]
    unnamed x4 -> x2, local copies, waits for them, and re-layouts: 0.01 us -> 2.67 us
  transfers between devices with their start and end apart: 2 -> 0, of which waited for: 2 -> 0; matrix products, arithmetic and copies ran while one was open for 1% -> 0% of each run, Pallas kernels for 0% -> 0%
where the time goes in v1:
time: 97.6 us; the launch traced here: 97.4 us
  Pallas kernels  92.3 us (95%)
  local copies, waits for them, and re-layouts  2.67 us (3%)
  between operations  2.39 us (2%)
    pallas_call x1, Pallas kernels, body(): pl.pallas_call(kernel, out_shape=(jax.ShapeDtypeStruct((ROWS, BS), F32),...  92.3 us
    unnamed x2, local copies, waits for them, and re-layouts  2.67 us

profile of v1, /device:TPU:32, one launch (start us, length us, event | category | flops | bytes accessed | tf_op | source)
XLA Modules:
  0.0 97.4 jit_solution(10129371956229457458)
XLA Ops:
  0.6 1.3 %copy_bitcast_fusion = (s32[6,32]{1,0:T(8,128)}, s32[6,32]{1,0:T(8,128)}) fusion(s32[1,6,32]{2,0,1:T(1,128)} %param.13, s32[1,6,32]{2,0,1:T(1,128)} %param.12), kind=kLoop, calls=%fused_computation | loop fusion | bytes 3072
  1.9 92.3 %shard_map.86 = (f32[64,128]{1,0:T(8,128)}, f32[1]{0:T(128)}) custom-call(bf16[64,128]{1,0:T(8,128)(2,1)} %amat_h.1, f32[1,64]{1,0:T(1,128)} %bitcast.9, f32[64,128]{1,0:T(8,128)} %hdiag_h.1, bf16[6,32,128,128]{3,2,1,0:T(8,128)(2,1)} %bitcast.7, bf16[6,32,128,128]{3,2,1,0:T(8,128)(2,1)} %bitcast.8, s32[6,32]{1,0:T(8,128)} %get-tuple-element.3.couple, ...), custom_call_target="tpu_custom_call" | custom-call | tf_op jit(solution)/shard_map/pallas_call | solution.py:396
  94.2 1.4 %copy.15 = f32[64,128]{1,0:T(8,128)} copy(f32[64,128]{1,0:T(8,128)} %get-tuple-element.6) | data formatting | bytes 65536

commit v2 on v1

--- a/solution.py
+++ b/solution.py
@@ -11,18 +11,17 @@
 NXZ = NX * NZ
 NSEG = 4
 NQ, BS, ROWS = 32, 128, 64
-UNIT = 4
-LAG = 6
+UNIT = GROUPS = 4
 F32, BF16 = jnp.float32, jnp.bfloat16
 
 
 def kernel(amat_h, lam_h, hdiag_h, left_h, right_h, couple, mask,
            out, theta_out,
            amat, lam, hdiag, left, right, lam_in, v, opp_send, near_send,
-           opp_in, near_in, own_acc, plane_send, plane_in, sigma,
+           opp_in, near_in, own_acc, work, plane_send, plane_in, sigma,
            numer, denom, numer_y, numer_p,
            load_sem, lam_sem, op_sem, lam_send, plane_s, plane_r,
-           ring_s, ring_r, last_s, last_r, sum_s, sum_r, psum_s, psum_r,
+           ring_s, ring_r, opp_s, opp_r, near_s, near_r, psum_s, psum_r,
            num_s, num_r, nump_s, nump_r):
     nterms = left.shape[0]
     seg = lax.axis_index("seg")
@@ -119,15 +118,10 @@
             where = piece(vec, device(tx, y, tz))
             return remote(where, where, ring_s.at[1, p], ring_r.at[1, s, tx * NZ + tz], device(x, down, z))
 
-        def on_up(p):
-            tx, tz = place(p)
-            where = piece(vec, device(tx, down, tz))
-            return remote(where, where, last_s.at[p], last_r.at[s, tx * NZ + tz], device(x, up, z))
-
-        def on_down(p):
-            tx, tz = place(p)
-            where = piece(vec, device(tx, up, tz))
-            return remote(where, where, last_s.at[p], last_r.at[s, tx * NZ + tz], device(x, down, z))
+        def pass_across(p):
+            tx, tz = place(p)
+            where = piece(vec, device(tx, y, tz))
+            return remote(where, where, ring_s.at[2, p], ring_r.at[2, s, tx * NZ + tz], device(x, across, z))
 
         def first(p, c):
             scatter_copy(p).start()
@@ -136,41 +130,20 @@
         lax.fori_loop(1, NXZ, first, 0)
 
         def hop(p, c):
-            @pl.when(p < NXZ)
+            @pl.when(p > 0)
             def _():
-                @pl.when(p > 0)
-                def _():
-                    arrival(p, y, plane_r).wait_recv()
-                pass_up(p).start()
-                pass_down(p).start()
-
-            @pl.when(p >= LAG)
-            def _():
-                q = p - LAG
-
-                @pl.when((q // 2) % 2 == 0)
-                def _():
-                    arrival(q, down, ring_r.at[0]).wait_recv()
-                    on_up(q).start()
-
-                @pl.when((q // 2) % 2 == 1)
-                def _():
-                    arrival(q, up, ring_r.at[1]).wait_recv()
-                    on_down(q).start()
-            return c
-
-        lax.fori_loop(0, NXZ + LAG, hop, 0)
+                arrival(p, y, plane_r).wait_recv()
+            pass_up(p).start()
+            pass_down(p).start()
+            pass_across(p).start()
+            return c
+
+        lax.fori_loop(0, NXZ, hop, 0)
 
         def finish(p, c):
-            @pl.when((p // 2) % 2 == 0)
-            def _():
-                arrival(p, up, ring_r.at[1]).wait_recv()
-
-            @pl.when((p // 2) % 2 == 1)
-            def _():
-                arrival(p, down, ring_r.at[0]).wait_recv()
-
-            arrival(p, across, last_r).wait_recv()
+            arrival(p, down, ring_r.at[0]).wait_recv()
+            arrival(p, up, ring_r.at[1]).wait_recv()
+            arrival(p, across, ring_r.at[2]).wait_recv()
             return c
 
         lax.fori_loop(0, NXZ, finish, 0)
@@ -181,7 +154,7 @@
                 scatter_copy(p).wait_send()
             pass_up(p).wait_send()
             pass_down(p).wait_send()
-            on_up(p).wait_send()
+            pass_across(p).wait_send()
             return c
 
         return functools.partial(lax.fori_loop, 0, NXZ, sent, 0)
@@ -191,8 +164,8 @@
     def block(s, i):
         inner = []
         for k in range(nterms):
-            live = mask[k, i]
-            j = couple[k, i] * live + NQ * (1 - live)
+            live = mask[k, 0, i]
+            j = couple[k, 0, i] * live + NQ * (1 - live)
             inner.append(jnp.dot(left[k, i], v[s, j], preferred_element_type=F32).astype(BF16))
         total = None
         for k in range(0, nterms, 2):
@@ -206,89 +179,99 @@
             denom[...] += jnp.sum((here * here).reshape(BS // 8, 8, BS), axis=0)
         return total
 
-    def unit(s, half, ty, keep):
-        base = half * (NQ // 2) + ty * UNIT
-
-        def step(b, c):
-            for b2 in range(2):
-                keep(2 * b + b2, block(s, base + 2 * b + b2))
-            return c
-
-        lax.fori_loop(0, UNIT // 2, step, 0)
+    def block_of(half, ty, g):
+        return half * (NQ // 2) + ty * UNIT + (z // 2 + (2 - g) * (g < 2) + 3 * (g == 2)) % UNIT
+
+    def unit(s, ty, g):
+        return [block(s, block_of(half, ty, g)) for half in range(NX)]
 
     def reduce(s):
+        def opp_copy(g):
+            target = device(x, (y + 1 + 2 * (g % 2)) % NY, z)
+            return remote(opp_send.at[g], opp_in.at[s, g], opp_s.at[g], opp_r.at[s, g], target)
+
+        def near_copy(d, g):
+            target = device(x, (y + 1 + 2 * d) % NY, z)
+            return remote(near_send.at[d, g], near_in.at[s, d, g], near_s.at[d, g], near_r.at[s, d, g], target)
+
+        def opposite(n, c):
+            groups = (2 * n, 2 * n + 1)
+            totals = [unit(s, across, g) for g in groups]
+            for g, both in zip(groups, totals):
+                for half in range(NX):
+                    opp_send[g, half] = both[half].astype(BF16)
+                opp_copy(g).start()
+            return c
+
+        lax.fori_loop(0, GROUPS // 2, opposite, 0)
+
+        def passed(g):
+            d = g % 2
+            opp_copy(g).wait_recv()
+            for half in range(NX):
+                near_send[d, g, half] = (work[d, g, half] + opp_in[s, g, half].astype(F32)).astype(BF16)
+            near_copy(d, g).start()
+
+        def near(g, c):
+            totals = [unit(s, other, g) for other in (up, down)]
+            for d in range(2):
+                for half in range(NX):
+                    work[d, g, half] = totals[d][half]
+            d = 1 - g % 2
+            for half in range(NX):
+                near_send[d, g, half] = work[d, g, half].astype(BF16)
+            near_copy(d, g).start()
+
+            @pl.when(g >= 2)
+            def _():
+                passed(g - 2)
+            return c
+
+        lax.fori_loop(0, GROUPS, near, 0)
+
+        def plane_copy(o):
+            return remote(plane_send.at[o], plane_in.at[s, xz], psum_s.at[o], psum_r.at[s, xz],
+                          device(o // NZ, y, o % NZ))
+
+        def pass_on(g):
+            for d in range(2):
+                near_copy(d, g).wait_recv()
+            first = block_of(0, 0, g)
+            for half in range(NX):
+                total = own_acc[g, half] + near_in[s, 0, g, half].astype(F32) + near_in[s, 1, g, half].astype(F32)
+                own_acc[g, half] = total
+                for side in range(2):
+                    plane_send[half * NZ + 2 * first + side] = total[side * ROWS:(side + 1) * ROWS].astype(BF16)
+            for half in range(NX):
+                for side in range(2):
+                    o = half * NZ + 2 * first + side
+
+                    @pl.when(o != xz)
+                    def _():
+                        plane_copy(o).start()
+
+        def own(n, c):
+            groups = (2 * n, 2 * n + 1)
+            totals = [unit(s, y, g) for g in groups]
+            for g, both in zip(groups, totals):
+                for half in range(NX):
+                    own_acc[g, half] = both[half]
+            passed(2 + n)
+            return c
+
+        lax.fori_loop(0, GROUPS // 2, own, 0)
+
         sends = []
-
-        def send(src, dst, index, target):
-            copy = remote(src, dst, sum_s.at[index], sum_r.at[s, index], device(x, target, z))
-            copy.start()
-            sends.append(copy)
-
-        def got(dst, index):
-            remote(dst, dst, sum_s.at[index], sum_r.at[s, index], device(x, up, z)).wait_recv()
-
-        def to(ref, *at):
-            def keep(b, total):
-                ref[(*at, b)] = total.astype(ref.dtype)
-            return keep
-
-        def plus(ref, add, at, add_at):
-            def keep(b, total):
-                ref[(*at, b)] = (total + add[(*add_at, b)].astype(F32)).astype(ref.dtype)
-            return keep
-
-        unit(s, 0, across, to(opp_send, 0))
-        send(opp_send.at[0], opp_in.at[s, 0], 0, up)
-        unit(s, 1, across, to(opp_send, 1))
-        send(opp_send.at[1], opp_in.at[s, 1], 1, down)
-        unit(s, 1, up, to(near_send, 0, 1))
-        send(near_send.at[0, 1], near_in.at[s, 0, 1], 2, up)
-        unit(s, 0, down, to(near_send, 1, 0))
-        send(near_send.at[1, 0], near_in.at[s, 1, 0], 3, down)
-        got(opp_in.at[s, 0], 0)
-        unit(s, 0, up, plus(near_send, opp_in, (0, 0), (s, 0)))
-        send(near_send.at[0, 0], near_in.at[s, 0, 0], 4, up)
-        got(opp_in.at[s, 1], 1)
-        unit(s, 1, down, plus(near_send, opp_in, (1, 1), (s, 1)))
-        send(near_send.at[1, 1], near_in.at[s, 1, 1], 5, down)
-        unit(s, 0, y, to(own_acc, 0))
-        unit(s, 1, y, to(own_acc, 1))
-
         if s == 0:
-            own = psi.astype(F32)
-            numer[...] += jnp.sum((hdiag[...] * own * own).reshape(ROWS // 8, 8, BS), axis=0)
+            start = psi.astype(F32)
+            numer[...] += jnp.sum((hdiag[...] * start * start).reshape(ROWS // 8, 8, BS), axis=0)
             numer_y[y] = numer[...]
             for n, other in enumerate((up, down, across)):
                 copy = remote(numer, numer_y.at[y], num_s.at[n], num_r.at[y], device(x, other, z))
                 copy.start()
                 sends.append(copy)
 
-        def plane_copy(half, t):
-            o = half * NZ + t
-            return remote(plane_send.at[half, t], plane_in.at[s, xz], psum_s.at[o], psum_r.at[s, xz],
-                          device(half, y, t))
-
-        for half in range(2):
-            got(near_in.at[s, 0, half], 4 if half == 0 else 2)
-            got(near_in.at[s, 1, half], 3 if half == 0 else 5)
-
-            def add(b, c):
-                total = (own_acc[half, b] + near_in[s, 0, half, b].astype(F32)
-                         + near_in[s, 1, half, b].astype(F32))
-                own_acc[half, b] = total
-                plane_send[half, 2 * b] = total[:ROWS].astype(BF16)
-                plane_send[half, 2 * b + 1] = total[ROWS:].astype(BF16)
-                return c
-
-            lax.fori_loop(0, UNIT, add, 0)
-
-            def go(t, c):
-                @pl.when(half * NZ + t != xz)
-                def _():
-                    plane_copy(half, t).start()
-                return c
-
-            lax.fori_loop(0, NZ, go, 0)
+        lax.fori_loop(0, GROUPS // 2, lambda g, c: (pass_on(g), c)[1], 0)
 
         if s == 0:
             for other in (up, down, across):
@@ -305,7 +288,9 @@
 
             lax.fori_loop(1, NXZ, go_numer, 0)
 
-        sigma[...] = own_acc[x, z // 2, pl.ds(pl.multiple_of((z % 2) * ROWS, ROWS), ROWS), :]
+        lax.fori_loop(GROUPS // 2, GROUPS, lambda g, c: (pass_on(g), c)[1], 0)
+
+        sigma[...] = own_acc[GROUPS - 1, x, pl.ds(pl.multiple_of((z % 2) * ROWS, ROWS), ROWS), :]
 
         def take(p, c):
             tx, tz = place(p)
@@ -330,10 +315,18 @@
             for copy in sends:
                 copy.wait_send()
 
+            def sent_ring(g, c):
+                opp_copy(g).wait_send()
+                near_copy(0, g).wait_send()
+                near_copy(1, g).wait_send()
+                return c
+
+            lax.fori_loop(0, GROUPS, sent_ring, 0)
+
             def sent(o, c):
                 @pl.when(o != xz)
                 def _():
-                    plane_copy(o // NZ, o % NZ).wait_send()
+                    plane_copy(o).wait_send()
                 return c
 
             lax.fori_loop(0, NXZ, sent, 0)
@@ -377,18 +370,17 @@
         vmem((terms, NQ, BS, BS), BF16), vmem((terms, NQ, BS, BS), BF16),
         vmem((1, ROWS), F32),
         vmem((2, NQ + 1, BS, BS), BF16),
-        vmem((2, UNIT, BS, BS), BF16), vmem((2, 2, UNIT, BS, BS), BF16),
-        vmem((2, 2, UNIT, BS, BS), BF16), vmem((2, 2, 2, UNIT, BS, BS), BF16),
-        vmem((2, UNIT, BS, BS), F32),
-        vmem((2, NZ, ROWS, BS), BF16), vmem((2, NXZ, ROWS, BS), BF16),
+        vmem((GROUPS, NX, BS, BS), BF16), vmem((2, GROUPS, NX, BS, BS), BF16),
+        vmem((2, GROUPS, NX, BS, BS), BF16), vmem((2, 2, GROUPS, NX, BS, BS), BF16),
+        vmem((GROUPS, NX, BS, BS), F32), vmem((2, GROUPS, NX, BS, BS), F32),
+        vmem((NXZ, ROWS, BS), BF16), vmem((2, NXZ, ROWS, BS), BF16),
         vmem((ROWS, BS), F32),
         vmem((8, BS), F32), vmem((8, BS), F32),
         vmem((NY, 8, BS), F32), vmem((NXZ, 8, BS), F32),
         dma((3,)), dma, dma((2, terms)), dma,
         dma((NXZ,)), dma((2, NXZ)),
-        dma((2, NXZ)), dma((2, 2, NXZ)),
-        dma((NXZ,)), dma((2, NXZ)),
-        dma((6,)), dma((2, 6)),
+        dma((3, NXZ)), dma((3, 2, NXZ)),
+        dma((GROUPS,)), dma((2, GROUPS)), dma((2, GROUPS)), dma((2, 2, GROUPS)),
         dma((NXZ,)), dma((2, NXZ)),
         dma((3,)), dma((NY,)),
         dma((NXZ,)), dma((NXZ,)),
@@ -402,7 +394,7 @@
         compiler_params=pltpu.CompilerParams(collective_id=0, has_side_effects=True),
     )(amat, lam.reshape(1, ROWS), hdiag,
       left_ops.reshape(terms, NQ, BS, BS), right_operators.reshape(terms, NQ, BS, BS),
-      couple[0], blockmask[0])
+      couple.reshape(terms, 1, NQ), blockmask.reshape(terms, 1, NQ))
     return sigma_two, theta
 
 

time: 97.6 us -> 89.7 us (0.919)
  Pallas kernels: 92.3 us -> 84.9 us
  local copies, waits for them, and re-layouts: 2.67 us -> 1.38 us
    pallas_call x1, Pallas kernels: 92.3 us -> 84.9 us  [body(): pl.pallas_call(kernel, out_shape=(jax.ShapeDtypeStruct((ROWS, BS), F32),...]
    unnamed x2 -> x1, local copies, waits for them, and re-layouts: 2.67 us -> 1.38 us
where the time goes in v2:
time: 89.7 us; the launch traced here: 88.7 us
  Pallas kernels  84.9 us (95%)
  between operations  2.4 us (3%)
  local copies, waits for them, and re-layouts  1.38 us (2%)
    pallas_call x1, Pallas kernels, body(): pl.pallas_call(kernel, out_shape=(jax.ShapeDtypeStruct((ROWS, BS), F32),...  84.9 us

profile of v2, /device:TPU:32, one launch (start us, length us, event | category | flops | bytes accessed | tf_op | source)
XLA Modules:
  0.0 88.7 jit_solution(6380238152946945872)
XLA Ops:
  0.6 84.9 %shard_map.86 = (f32[64,128]{1,0:T(8,128)}, f32[1]{0:T(128)}) custom-call(bf16[64,128]{1,0:T(8,128)(2,1)} %amat_h.1, f32[1,64]{1,0:T(1,128)} %bitcast.9, f32[64,128]{1,0:T(8,128)} %hdiag_h.1, bf16[6,32,128,128]{3,2,1,0:T(8,128)(2,1)} %bitcast.5, bf16[6,32,128,128]{3,2,1,0:T(8,128)(2,1)} %bitcast.6, s32[6,1,32]{2,1,0:T(1,128)} %bitcast.7, s32[6,1,32]{2,1,0:T(1,128)} %bitcast.8), custom_call_target="tpu_custom_call" | custom-call | tf_op jit(solution)/shard_map/pallas_call | solution.py:388
  85.6 1.4 %copy.11 = f32[64,128]{1,0:T(8,128)} copy(f32[64,128]{1,0:T(8,128)} %get-tuple-element.4) | data formatting | bytes 65536

commit v3 on v2

--- a/solution.py
+++ b/solution.py
@@ -12,6 +12,7 @@
 NSEG = 4
 NQ, BS, ROWS = 32, 128, 64
 UNIT = GROUPS = 4
+CROSS_LAG = 4
 F32, BF16 = jnp.float32, jnp.bfloat16
 
 
@@ -19,7 +20,7 @@
            out, theta_out,
            amat, lam, hdiag, left, right, lam_in, v, opp_send, near_send,
            opp_in, near_in, own_acc, work, plane_send, plane_in, sigma,
-           numer, denom, numer_y, numer_p,
+           numer, denom, numer_row, numer_y, numer_p,
            load_sem, lam_sem, op_sem, lam_send, plane_s, plane_r,
            ring_s, ring_r, opp_s, opp_r, near_s, near_r, psum_s, psum_r,
            num_s, num_r, nump_s, nump_r):
@@ -123,22 +124,40 @@
             where = piece(vec, device(tx, y, tz))
             return remote(where, where, ring_s.at[2, p], ring_r.at[2, s, tx * NZ + tz], device(x, across, z))
 
-        def first(p, c):
-            scatter_copy(p).start()
-            return c
-
-        lax.fori_loop(1, NXZ, first, 0)
-
-        def hop(p, c):
-            @pl.when(p > 0)
-            def _():
-                arrival(p, y, plane_r).wait_recv()
+        def cross(n):
+            tz = place(2 * n)[1]
+            where = piece(vec, device(x, y, tz))
+            return remote(where, where, plane_s.at[2 * n + 1], plane_r.at[s, x * NZ + tz], device(1 - x, y, z))
+
+        def first(n, c):
+            scatter_copy(2 * n).start()
+            return c
+
+        cross(0).start()
+        lax.fori_loop(1, NZ, first, 0)
+
+        def fan(p):
             pass_up(p).start()
             pass_down(p).start()
             pass_across(p).start()
-            return c
-
-        lax.fori_loop(0, NXZ, hop, 0)
+
+        def hop(n, c):
+            @pl.when(n < NZ)
+            def _():
+                @pl.when(n > 0)
+                def _():
+                    arrival(2 * n, y, plane_r).wait_recv()
+                    cross(n).start()
+                fan(2 * n)
+
+            @pl.when(n >= CROSS_LAG)
+            def _():
+                p = 2 * (n - CROSS_LAG) + 1
+                arrival(p, y, plane_r).wait_recv()
+                fan(p)
+            return c
+
+        lax.fori_loop(0, NZ + CROSS_LAG, hop, 0)
 
         def finish(p, c):
             arrival(p, down, ring_r.at[0]).wait_recv()
@@ -195,7 +214,7 @@
             return remote(near_send.at[d, g], near_in.at[s, d, g], near_s.at[d, g], near_r.at[s, d, g], target)
 
         def opposite(n, c):
-            groups = (2 * n, 2 * n + 1)
+            groups = tuple(range(GROUPS))
             totals = [unit(s, across, g) for g in groups]
             for g, both in zip(groups, totals):
                 for half in range(NX):
@@ -203,7 +222,7 @@
                 opp_copy(g).start()
             return c
 
-        lax.fori_loop(0, GROUPS // 2, opposite, 0)
+        lax.fori_loop(0, 1, opposite, 0)
 
         def passed(g):
             d = g % 2
@@ -212,22 +231,22 @@
                 near_send[d, g, half] = (work[d, g, half] + opp_in[s, g, half].astype(F32)).astype(BF16)
             near_copy(d, g).start()
 
-        def near(g, c):
-            totals = [unit(s, other, g) for other in (up, down)]
-            for d in range(2):
+        def near(n, c):
+            totals = [[unit(s, other, 2 * n + e) for other in (up, down)] for e in range(2)]
+            for e in range(2):
+                g = 2 * n + e
                 for half in range(NX):
-                    work[d, g, half] = totals[d][half]
-            d = 1 - g % 2
-            for half in range(NX):
-                near_send[d, g, half] = work[d, g, half].astype(BF16)
-            near_copy(d, g).start()
-
-            @pl.when(g >= 2)
+                    work[e, g, half] = totals[e][e][half]
+                    near_send[1 - e, g, half] = totals[e][1 - e][half].astype(BF16)
+                near_copy(1 - e, g).start()
+
+            @pl.when(n >= 1)
             def _():
-                passed(g - 2)
-            return c
-
-        lax.fori_loop(0, GROUPS, near, 0)
+                passed(0)
+                passed(1)
+            return c
+
+        lax.fori_loop(0, GROUPS // 2, near, 0)
 
         def plane_copy(o):
             return remote(plane_send.at[o], plane_in.at[s, xz], psum_s.at[o], psum_r.at[s, xz],
@@ -251,23 +270,25 @@
                         plane_copy(o).start()
 
         def own(n, c):
-            groups = (2 * n, 2 * n + 1)
+            groups = tuple(range(GROUPS))
             totals = [unit(s, y, g) for g in groups]
             for g, both in zip(groups, totals):
                 for half in range(NX):
                     own_acc[g, half] = both[half]
-            passed(2 + n)
-            return c
-
-        lax.fori_loop(0, GROUPS // 2, own, 0)
+            passed(2)
+            passed(3)
+            return c
+
+        lax.fori_loop(0, 1, own, 0)
 
         sends = []
         if s == 0:
             start = psi.astype(F32)
             numer[...] += jnp.sum((hdiag[...] * start * start).reshape(ROWS // 8, 8, BS), axis=0)
-            numer_y[y] = numer[...]
+            numer_row[...] = jnp.sum(numer[...], axis=0, keepdims=True)
+            numer_y[y] = numer_row[...]
             for n, other in enumerate((up, down, across)):
-                copy = remote(numer, numer_y.at[y], num_s.at[n], num_r.at[y], device(x, other, z))
+                copy = remote(numer_row, numer_y.at[y], num_s.at[n], num_r.at[y], device(x, other, z))
                 copy.start()
                 sends.append(copy)
 
@@ -275,7 +296,7 @@
 
         if s == 0:
             for other in (up, down, across):
-                remote(numer, numer_y.at[other], num_s.at[0], num_r.at[other], device(x, up, z)).wait_recv()
+                remote(numer_row, numer_y.at[other], num_s.at[0], num_r.at[other], device(x, up, z)).wait_recv()
             numer_p[xz] = (numer_y[0] + numer_y[1]) + (numer_y[2] + numer_y[3])
 
             def numer_copy(p):
@@ -376,7 +397,7 @@
         vmem((NXZ, ROWS, BS), BF16), vmem((2, NXZ, ROWS, BS), BF16),
         vmem((ROWS, BS), F32),
         vmem((8, BS), F32), vmem((8, BS), F32),
-        vmem((NY, 8, BS), F32), vmem((NXZ, 8, BS), F32),
+        vmem((1, BS), F32), vmem((NY, 1, BS), F32), vmem((NXZ, 1, BS), F32),
         dma((3,)), dma, dma((2, terms)), dma,
         dma((NXZ,)), dma((2, NXZ)),
         dma((3, NXZ)), dma((3, 2, NXZ)),

time: 89.7 us -> 86.3 us (0.962)
  Pallas kernels: 84.9 us -> 82.2 us
    pallas_call x1, Pallas kernels: 84.9 us -> 82.2 us  [body(): pl.pallas_call(kernel, out_shape=(jax.ShapeDtypeStruct((ROWS, BS), F32),...]
where the time goes in v3:
time: 86.3 us; the launch traced here: 86 us
  Pallas kernels  82.2 us (95%)
  between operations  2.4 us (3%)
  local copies, waits for them, and re-layouts  1.38 us (2%)
    pallas_call x1, Pallas kernels, body(): pl.pallas_call(kernel, out_shape=(jax.ShapeDtypeStruct((ROWS, BS), F32),...  82.2 us

profile of v3, /device:TPU:32, one launch (start us, length us, event | category | flops | bytes accessed | tf_op | source)
XLA Modules:
  0.0 86.0 jit_solution(1492163545193020997)
XLA Ops:
  0.6 82.2 %shard_map.86 = (f32[64,128]{1,0:T(8,128)}, f32[1]{0:T(128)}) custom-call(bf16[64,128]{1,0:T(8,128)(2,1)} %amat_h.1, f32[1,64]{1,0:T(1,128)} %bitcast.9, f32[64,128]{1,0:T(8,128)} %hdiag_h.1, bf16[6,32,128,128]{3,2,1,0:T(8,128)(2,1)} %bitcast.5, bf16[6,32,128,128]{3,2,1,0:T(8,128)(2,1)} %bitcast.6, s32[6,1,32]{2,1,0:T(1,128)} %bitcast.7, s32[6,1,32]{2,1,0:T(1,128)} %bitcast.8), custom_call_target="tpu_custom_call" | custom-call | tf_op jit(solution)/shard_map/pallas_call | solution.py:409
  82.8 1.4 %copy.11 = f32[64,128]{1,0:T(8,128)} copy(f32[64,128]{1,0:T(8,128)} %get-tuple-element.4) | data formatting | bytes 65536

commit v4 on v3

--- a/solution.py
+++ b/solution.py
@@ -137,9 +137,9 @@
         lax.fori_loop(1, NZ, first, 0)
 
         def fan(p):
+            pass_across(p).start()
             pass_up(p).start()
             pass_down(p).start()
-            pass_across(p).start()
 
         def hop(n, c):
             @pl.when(n < NZ)

time: 86.3 us -> 85.8 us (level)
  no operation moved by 1% of the time
where the time goes in v4:
time: 85.8 us; the launch traced here: 85.2 us
  Pallas kernels  81.4 us (95%)
  between operations  2.4 us (3%)
  local copies, waits for them, and re-layouts  1.38 us (2%)
    pallas_call x1, Pallas kernels, body(): pl.pallas_call(kernel, out_shape=(jax.ShapeDtypeStruct((ROWS, BS), F32),...  81.4 us

profile of v4, /device:TPU:32, one launch (start us, length us, event | category | flops | bytes accessed | tf_op | source)
XLA Modules:
  0.0 85.2 jit_solution(14828951423435630425)
XLA Ops:
  0.6 81.4 %shard_map.86 = (f32[64,128]{1,0:T(8,128)}, f32[1]{0:T(128)}) custom-call(bf16[64,128]{1,0:T(8,128)(2,1)} %amat_h.1, f32[1,64]{1,0:T(1,128)} %bitcast.9, f32[64,128]{1,0:T(8,128)} %hdiag_h.1, bf16[6,32,128,128]{3,2,1,0:T(8,128)(2,1)} %bitcast.5, bf16[6,32,128,128]{3,2,1,0:T(8,128)(2,1)} %bitcast.6, s32[6,1,32]{2,1,0:T(1,128)} %bitcast.7, s32[6,1,32]{2,1,0:T(1,128)} %bitcast.8), custom_call_target="tpu_custom_call" | custom-call | tf_op jit(solution)/shard_map/pallas_call | solution.py:409
  82.1 1.4 %copy.11 = f32[64,128]{1,0:T(8,128)} copy(f32[64,128]{1,0:T(8,128)} %get-tuple-element.4) | data formatting | bytes 65536
